TPU v7x, 32 devices: a whole 2x2x4 slice. The times are simulated.
32 devices in a mesh: row: 4 (over x, core), col: 8 (over z, y).
Axes of the slice: x: 2, y: 2, z: 4, core: 2. Of those that a mesh axis runs over, the one named last changes fastest.
Arguments:
- points: float32 [16, 8192], P(None, ('row', 'col')), may hold values from -6 to 6
- lengthscale: float32 [16], replicated, may hold values from 2 to 8
- signal: float32 [1], replicated, may hold values from 0.5 to 2
- noise: float32 [1], replicated, may hold values from 0.05 to 0.5
- targets: float32 [8192], P(('row', 'col')), may hold values from -12 to 12
- probe_bits: int32 [31, 8192], P(None, ('row', 'col')), may hold values from 0 to 1
Outputs:
- solution: float32 [32, 8192], P(None, ('row', 'col'))
- residual: float32 [32, 8192], P(None, ('row', 'col'))
All inputs are finite; a program needn't handle non-finite values.
Results may differ from a plain program's by a relative error of at most 0.0013.
Values sent between devices are 32-bit elements; how exact they have to be, the bound alone decides.
No kernel may reach another device: no remote copies, remote signals or barrier semaphores. Data moves between devices by JAX's collectives and lax.ppermute only.
A program may use at most 128 MiB of HBM per device.

v0:
```python
import jax
import jax.numpy as jnp
from jax import lax
from jax.sharding import PartitionSpec as P

ITERS = 3
ROOT_FIVE = 5.0**0.5


def matern_tile(row_scaled, col_scaled, signal_value):
    row_sq = jnp.sum(row_scaled * row_scaled, axis=0)
    col_sq = jnp.sum(col_scaled * col_scaled, axis=0)
    cross_term = lax.dot_general(
        row_scaled,
        col_scaled,
        (((0,), (0,)), ((), ())),
        precision=lax.Precision.HIGHEST,
        preferred_element_type=jnp.float32,
    )
    dist_sq = jnp.maximum(row_sq[:, None] + col_sq[None, :] - 2.0 * cross_term, 0.0)
    radius = jnp.sqrt(dist_sq)
    return (
        signal_value
        * (1.0 + ROOT_FIVE * radius + 5.0 / 3.0 * dist_sq)
        * jnp.exp(-ROOT_FIVE * radius)
    )


def row_blocks(row_scaled):
    row_total = row_scaled.shape[1]
    block_rows = min(1024, row_total)
    block_count = row_total // block_rows
    return row_scaled.reshape(row_scaled.shape[0], block_count, block_rows).transpose(1, 0, 2)


def apply_tile(row_scaled, col_scaled, signal_value, vectors):
    row_total = row_scaled.shape[1]
    stacked = row_blocks(row_scaled)

    def one_block(row_block):
        kernel_tile = matern_tile(row_block, col_scaled, signal_value)
        return lax.dot_general(
            vectors,
            kernel_tile,
            (((1,), (1,)), ((), ())),
            precision=lax.Precision.HIGHEST,
            preferred_element_type=jnp.float32,
        )

    pieces = lax.map(one_block, stacked)
    return pieces.transpose(1, 0, 2).reshape(vectors.shape[0], row_total)


def squares(residual):
    return lax.psum(jnp.sum(residual * residual, axis=1), ("row", "col"))


def body(points, lengthscale, signal, noise, targets, probe_bits):
    scaled = points / lengthscale[:, None]
    signs = 2.0 * probe_bits.astype(jnp.float32) - 1.0
    right_side = jnp.concatenate([targets[None, :], signs], axis=0)
    signal_value = signal[0]
    noise_value = noise[0]
    every_point = lax.all_gather(scaled, ("row", "col"), axis=1, tiled=True)
    solution = jnp.zeros_like(right_side)
    residual = right_side
    direction = right_side
    norm_now = squares(residual)
    for step in range(ITERS):
        summed = apply_tile(
            scaled,
            every_point,
            signal_value,
            lax.all_gather(direction, ("row", "col"), axis=1, tiled=True),
        )
        image = summed + noise_value * direction
        curved = lax.psum(jnp.sum(direction * image, axis=1), ("row", "col"))
        alpha = norm_now / curved
        solution = solution + alpha[:, None] * direction
        residual = residual - alpha[:, None] * image
        if step + 1 < ITERS:
            norm_next = squares(residual)
            direction = residual + (norm_next / norm_now)[:, None] * direction
            norm_now = norm_next
    return (solution, residual)


def solution(mesh):
    return jax.shard_map(
        body,
        mesh=mesh,
        in_specs=(
            P(None, ("row", "col")),
            P(),
            P(),
            P(),
            P(("row", "col")),
            P(None, ("row", "col")),
        ),
        out_specs=(P(None, ("row", "col")), P(None, ("row", "col"))),
        check_vma=False,
    )
```

profile of v0, /device:TPU:0, one launch (start us, length us, event | category | flops | bytes accessed | tf_op | source)
XLA Modules:
  0.0 442.8 jit_solution(3945853298160864915)
XLA Ops:
  7.2 0.0 all-gather.4.cloned.1.call-start
  7.2 0.8 multiply_add_fusion.3
  8.0 1.3 pad_maximum_fusion
  9.3 0.0 all-gather.4.cloned.1.call-update
  9.3 0.0 all-gather.6.cloned.1.call-start
  10.6 0.8 multiply_reduce_fusion.7
  11.5 73.2 %all_gather.13 = f32[16,8192]{1,0:T(8,128)S(1)} all-gather(f32[16,256]{1,0:T(8,128)S(1)} %get-tuple-element.51), channel_id=1, replica_groups=mesh['row'=4,'col'=8] {'row','col'}, dimensions={1}, use_global_device_ids=true | all-gather | bytes 540672 | tf_op jit(solution)/shard_map/all_gather | solution.py:64
  84.6 0.1 multiply_reduce_fusion
  84.7 0.0 copy-start.2
  84.7 14.0 %exponential_multiply_fusion = f32[256,8192]{1,0:T(8,128)} fusion(f32[16,256]{1,0:T(8,128)S(1)} %get-tuple-element.51, f32[16,8192]{1,0:T(8,128)S(1)} %all_gather.13, f32[8192]{0:T(1024)S(1)} %multiply_reduce_fusion, f32[256]{0:T(256)S(1)} %get-tuple-element.50, f32[]{:T(128)} %bitcast.11), kind=kOutput, calls=%fused_computation.3 | convolution fusion | flops 425721856 | bytes 8963076 | tf_op jit(solution)/shard_map/while/body/eval_jaxpr/dot_general | solution.py:13
  98.7 0.0 copy-start.3
  98.7 0.0 all-gather.4.cloned.1.call-done
  98.7 0.0 copy-done.2
  98.8 11.2 %multiply_reduce_fusion.5 = (f32[32]{0:T(128)S(1)}, f32[32]{0:T(128)S(1)}, f32[32,256]{1,0:T(8,128)S(1)}) fusion(f32[32,256]{1,0:T(8,128)S(1)} %copy-done.2, f32[]{:T(128)} %bitcast.12, f32[32,8192]{1,0:T(8,128)} %all-gather.4.cloned.1.call-done, f32[256,8192]{1,0:T(8,128)} %exponential_multiply_fusion), kind=kOutput, calls=%fused_computation.19 | convolution fusion | flops 805355456 | bytes 9502980 | tf_op jit(solution)/shard_map/while/body/eval_jaxpr/dot_general | solution.py:42
  109.9 37.1 %all-reduce = (f32[32]{0:T(128)S(1)}, f32[32]{0:T(128)S(1)}) all-reduce(f32[32]{0:T(128)S(1)} %get-tuple-element.39, f32[32]{0:T(128)S(1)} %get-tuple-element.38), channel_id=1, replica_groups=mesh['row'=4,'col'=8] {'row','col'}, use_global_device_ids=true, to_apply=%region_1.0 | all-reduce | flops 64 | bytes 512 | tf_op jit(solution)/shard_map/psum | solution.py:55
  147.0 0.0 copy-done.3
  147.0 0.2 multiply_reduce_fusion.4
  147.2 41.5 %psum.44 = f32[32]{0:T(128)S(1)} all-reduce(f32[32]{0:T(128)S(1)} %multiply_reduce_fusion.4), channel_id=1, replica_groups=mesh['row'=4,'col'=8] {'row','col'}, use_global_device_ids=true, to_apply=%region_7.8 | all-reduce | flops 32 | bytes 256 | tf_op jit(solution)/shard_map/psum | solution.py:55
  188.7 0.7 multiply_add_fusion.2
  189.4 0.0 copy-start
  189.4 0.0 all-gather.6.cloned.1.call-update
  189.5 0.0 all-gather.8.cloned.1.call-start
  189.5 51.3 %all-gather.6.cloned.1.call-done = f32[32,8192]{1,0:T(8,128)} async-done(((f32[32,256]{1,0:T(8,128)}), f32[32,8192]{1,0:T(8,128)}) %all-gather.6.cloned.1.call-update) | async-done | bytes 1048592 | tf_op jit(solution)/shard_map/all_gather | solution.py:74
  240.8 11.1 %multiply_reduce_fusion.3 = (f32[32]{0:T(128)S(1)}, f32[32,256]{1,0:T(8,128)S(1)}) fusion(f32[32,256]{1,0:T(8,128)} %multiply_add_fusion.2, f32[]{:T(128)} %bitcast.14, f32[32,8192]{1,0:T(8,128)} %all-gather.6.cloned.1.call-done, f32[256,8192]{1,0:T(8,128)} %exponential_multiply_fusion), kind=kOutput, calls=%fused_computation.15 | convolution fusion | flops 805339136 | bytes 9502852 | tf_op jit(solution)/shard_map/while/body/eval_jaxpr/dot_general | solution.py:42
  251.9 40.3 %psum.45 = f32[32]{0:T(128)S(1)} all-reduce(f32[32]{0:T(128)S(1)} %get-tuple-element.61), channel_id=1, replica_groups=mesh['row'=4,'col'=8] {'row','col'}, use_global_device_ids=true, to_apply=%region_9.10 | all-reduce | flops 32 | bytes 256 | tf_op jit(solution)/shard_map/psum | solution.py:77
  292.1 0.2 multiply_reduce_fusion.2
  292.3 39.2 %psum.46 = f32[32]{0:T(128)S(1)} all-reduce(f32[32]{0:T(128)S(1)} %get-tuple-element.48), channel_id=1, replica_groups=mesh['row'=4,'col'=8] {'row','col'}, use_global_device_ids=true, to_apply=%region_11.12 | all-reduce | flops 32 | bytes 256 | tf_op jit(solution)/shard_map/psum | solution.py:55
  331.5 0.0 copy-done
  331.5 0.7 multiply_add_fusion.1
  332.2 0.0 copy-start.1
  332.2 0.0 all-gather.8.cloned.1.call-update
  332.3 52.0 %all-gather.8.cloned.1.call-done = f32[32,8192]{1,0:T(8,128)} async-done(((f32[32,256]{1,0:T(8,128)}), f32[32,8192]{1,0:T(8,128)}) %all-gather.8.cloned.1.call-update) | async-done | bytes 1048592 | tf_op jit(solution)/shard_map/all_gather | solution.py:74
  384.2 11.1 %multiply_reduce_fusion.1 = (f32[32]{0:T(128)S(1)}, f32[32,256]{1,0:T(8,128)S(1)}) fusion(f32[32,256]{1,0:T(8,128)} %multiply_add_fusion.1, f32[]{:T(128)} %bitcast.13, f32[32,8192]{1,0:T(8,128)} %all-gather.8.cloned.1.call-done, f32[256,8192]{1,0:T(8,128)} %exponential_multiply_fusion), kind=kOutput, calls=%fused_computation.11 | convolution fusion | flops 805339136 | bytes 9502852 | tf_op jit(solution)/shard_map/while/body/eval_jaxpr/dot_general | solution.py:42
  395.3 40.3 %psum.47 = f32[32]{0:T(128)S(1)} all-reduce(f32[32]{0:T(128)S(1)} %get-tuple-element.63), channel_id=1, replica_groups=mesh['row'=4,'col'=8] {'row','col'}, use_global_device_ids=true, to_apply=%region_13.14 | all-reduce | flops 32 | bytes 256 | tf_op jit(solution)/shard_map/psum | solution.py:77
  435.5 0.0 copy-done.1
  435.5 0.7 multiply_subtract_fusion
  (5 shorter events, 0.0 us)
Async XLA Ops:
  7.2 91.6 %all-gather.4.cloned.1.call-start = ((), (), s32[]{:S(2)}) async-start(), calls=%async_computation | async-start | bytes 1081344 | tf_op jit(solution)/shard_map/all_gather | solution.py:74
  9.3 231.5 %all-gather.6.cloned.1.call-start = ((), (), s32[]{:S(2)}) async-start(), calls=%async_computation.1 | async-start | bytes 1081344 | tf_op jit(solution)/shard_map/all_gather | solution.py:74
  84.7 14.0 %copy-start.2 = (f32[32,256]{1,0:T(8,128)S(1)}, f32[32,256]{1,0:T(8,128)}, u32[]{:S(2)}) copy-start(f32[32,256]{1,0:T(8,128)} %pad_maximum_fusion) | copy-start | bytes 98308
  98.7 48.3 %copy-start.3 = (f32[256]{0:T(256)S(1)}, f32[256]{0:T(256)}, u32[]{:S(2)}) copy-start(f32[256]{0:T(256)} %param.10) | copy-start | bytes 3076
  189.4 142.1 %copy-start = (f32[32,256]{1,0:T(8,128)S(1)}, f32[32,256]{1,0:T(8,128)}, u32[]{:S(2)}) copy-start(f32[32,256]{1,0:T(8,128)} %multiply_add_fusion.2) | copy-start | bytes 98308
  189.5 194.7 %all-gather.8.cloned.1.call-start = ((), (), s32[]{:S(2)}) async-start(), calls=%async_computation.2 | async-start | bytes 1081344 | tf_op jit(solution)/shard_map/all_gather | solution.py:74
  332.2 103.3 %copy-start.1 = (f32[32,256]{1,0:T(8,128)S(1)}, f32[32,256]{1,0:T(8,128)}, u32[]{:S(2)}) copy-start(f32[32,256]{1,0:T(8,128)} %multiply_add_fusion.1) | copy-start | bytes 98308
Sparse Core Ops, SparseCore 0:
  11.4 54.6 all-gather.3
  189.6 51.1 all-gather.5
  332.4 51.7 all-gather.7
where the time goes:
time: 444 us; the launch traced here: 443 us
  blocking collectives  272 us (61%)
  waiting for transfers between devices  103 us (23%)
  matrix products  47.3 us (11%)
  between operations  15.1 us (3%)
  other arithmetic  5.46 us (1%)
    psum x3, blocking collectives, squares(): return lax.psum(jnp.sum(residual * residual, axis=1), ('row', 'col'))  118 us
    all_gather x3, waiting for transfers between devices, body(): lax.all_gather(direction, ('row', 'col'), axis=1, tiled=True)  103 us
    psum x2, blocking collectives, body(): curved = lax.psum(jnp.sum(direction * image, axis=1), ('row', 'col'))  80.5 us
    all_gather x1, blocking collectives, body(): every_point = lax.all_gather(scaled, ('row', 'col'), axis=1, tiled=True)  73.2 us
    dot_general x3, matrix products, one_block(): lax.dot_general(vectors, kernel_tile, (((1,), (1,)), ((), ())), precision...  33.3 us
    dot_general x1, matrix products, matern_tile(): lax.dot_general(row_scaled, col_scaled, (((0,), (0,)), ((), ())), precisi...  14 us
  transfers between devices with their start and end apart: 3, of which 2 were waited for; matrix products, arithmetic and copies ran while one was open for 3% of the time, Pallas kernels for 0%

commit v1 on v0

--- a/solution.py
+++ b/solution.py
@@ -71,7 +71,7 @@
             scaled,
             every_point,
             signal_value,
-            lax.all_gather(direction, ("row", "col"), axis=1, tiled=True),
+            jnp.concatenate(lax.all_gather(direction, ("row", "col")), axis=1),
         )
         image = summed + noise_value * direction
         curved = lax.psum(jnp.sum(direction * image, axis=1), ("row", "col"))

time: 444 us -> 446 us (level)
  no operation moved by 1% of the time
where the time goes in v1:
time: 446 us; the launch traced here: 445 us
  blocking collectives  270 us (61%)
  waiting for transfers between devices  107 us (24%)
  matrix products  43.5 us (10%)
  between operations  15.1 us (3%)
  other arithmetic  5.46 us (1%)
    psum x3, blocking collectives, squares(): return lax.psum(jnp.sum(residual * residual, axis=1), ('row', 'col'))  119 us
    all_gather x3, waiting for transfers between devices, body(): lax.all_gather(direction, ('row', 'col'))  107 us
    psum x2, blocking collectives, body(): curved = lax.psum(jnp.sum(direction * image, axis=1), ('row', 'col'))  78.6 us
    all_gather x1, blocking collectives, body(): every_point = lax.all_gather(scaled, ('row', 'col'), axis=1, tiled=True)  73 us
    dot_general x3, matrix products, one_block(): lax.dot_general(vectors, kernel_tile, (((1,), (1,)), ((), ())), precision...  29.5 us
    dot_general x1, matrix products, matern_tile(): lax.dot_general(row_scaled, col_scaled, (((0,), (0,)), ((), ())), precisi...  14 us
  transfers between devices with their start and end apart: 3, of which 2 were waited for; matrix products, arithmetic and copies ran while one was open for 3% of the time, Pallas kernels for 0%

profile of v1, /device:TPU:0, one launch (start us, length us, event | category | flops | bytes accessed | tf_op | source)
XLA Modules:
  0.0 445.3 jit_solution(10830313072789879165)
XLA Ops:
  7.2 0.0 all-gather.7.cloned.1.call-start
  7.2 0.8 multiply_add_fusion.3
  8.0 1.3 pad_maximum_fusion
  9.3 0.0 all-gather.7.cloned.1.call-update
  9.3 0.0 all-gather.9.cloned.1.call-start
  10.6 0.8 multiply_reduce_fusion.7
  11.5 73.0 %all_gather.19 = f32[16,8192]{1,0:T(8,128)S(1)} all-gather(f32[16,256]{1,0:T(8,128)S(1)} %get-tuple-element.51), channel_id=1, replica_groups=mesh['row'=4,'col'=8] {'row','col'}, dimensions={1}, use_global_device_ids=true | all-gather | bytes 540672 | tf_op jit(solution)/shard_map/all_gather | solution.py:64
  84.4 0.1 multiply_reduce_fusion
  84.5 0.0 copy-start.2
  84.5 14.0 %exponential_multiply_fusion = f32[256,8192]{1,0:T(8,128)} fusion(f32[16,256]{1,0:T(8,128)S(1)} %get-tuple-element.51, f32[16,8192]{1,0:T(8,128)S(1)} %all_gather.19, f32[8192]{0:T(1024)S(1)} %multiply_reduce_fusion, f32[256]{0:T(256)S(1)} %get-tuple-element.50, f32[]{:T(128)} %bitcast.29), kind=kOutput, calls=%fused_computation.3 | convolution fusion | flops 425721856 | bytes 8963076 | tf_op jit(solution)/shard_map/while/body/eval_jaxpr/dot_general | solution.py:13
  98.5 0.0 copy-start.3
  98.5 0.0 all-gather.7.cloned.1.call-done
  98.5 1.3 copy.11
  99.8 0.0 copy-done.2
  99.9 9.8 %multiply_reduce_fusion.5 = (f32[32]{0:T(128)S(1)}, f32[32]{0:T(128)S(1)}, f32[32,256]{1,0:T(8,128)S(1)}) fusion(f32[32,256]{1,0:T(8,128)S(1)} %copy-done.2, f32[]{:T(128)} %bitcast.30, f32[32,8192]{1,0:T(8,128)S(1)} %bitcast.33, f32[256,8192]{1,0:T(8,128)} %exponential_multiply_fusion), kind=kOutput, calls=%fused_computation.19 | convolution fusion | flops 805355456 | bytes 9502980 | tf_op jit(solution)/shard_map/while/body/eval_jaxpr/dot_general | solution.py:42
  109.7 36.9 %all-reduce = (f32[32]{0:T(128)S(1)}, f32[32]{0:T(128)S(1)}) all-reduce(f32[32]{0:T(128)S(1)} %get-tuple-element.39, f32[32]{0:T(128)S(1)} %get-tuple-element.38), channel_id=1, replica_groups=mesh['row'=4,'col'=8] {'row','col'}, use_global_device_ids=true, to_apply=%region_1.0 | all-reduce | flops 64 | bytes 512 | tf_op jit(solution)/shard_map/psum | solution.py:55
  146.6 0.0 copy-done.3
  146.6 0.2 multiply_reduce_fusion.4
  146.7 41.9 %psum.44 = f32[32]{0:T(128)S(1)} all-reduce(f32[32]{0:T(128)S(1)} %multiply_reduce_fusion.4), channel_id=1, replica_groups=mesh['row'=4,'col'=8] {'row','col'}, use_global_device_ids=true, to_apply=%region_7.8 | all-reduce | flops 32 | bytes 256 | tf_op jit(solution)/shard_map/psum | solution.py:55
  188.6 0.7 multiply_add_fusion.2
  189.3 0.0 copy-start
  189.3 0.0 all-gather.9.cloned.1.call-update
  189.3 0.2 all-gather.11.cloned.1.call-start
  189.6 53.1 %all-gather.9.cloned.1.call-done = f32[1024,256]{1,0:T(8,128)} async-done(((f32[32,256]{1,0:T(8,128)}), f32[1024,256]{1,0:T(8,128)}) %all-gather.9.cloned.1.call-update) | async-done | bytes 1048592 | tf_op jit(solution)/shard_map/all_gather | solution.py:74
  242.7 1.3 copy.12
  244.0 9.8 %multiply_reduce_fusion.3 = (f32[32]{0:T(128)S(1)}, f32[32,256]{1,0:T(8,128)S(1)}) fusion(f32[32,256]{1,0:T(8,128)} %multiply_add_fusion.2, f32[]{:T(128)} %bitcast.32, f32[32,8192]{1,0:T(8,128)S(1)} %bitcast.35, f32[256,8192]{1,0:T(8,128)} %exponential_multiply_fusion), kind=kOutput, calls=%fused_computation.15 | convolution fusion | flops 805339136 | bytes 9502852 | tf_op jit(solution)/shard_map/while/body/eval_jaxpr/dot_general | solution.py:42
  253.8 39.3 %psum.45 = f32[32]{0:T(128)S(1)} all-reduce(f32[32]{0:T(128)S(1)} %get-tuple-element.61), channel_id=1, replica_groups=mesh['row'=4,'col'=8] {'row','col'}, use_global_device_ids=true, to_apply=%region_9.10 | all-reduce | flops 32 | bytes 256 | tf_op jit(solution)/shard_map/psum | solution.py:77
  293.2 0.2 multiply_reduce_fusion.2
  293.4 39.8 %psum.46 = f32[32]{0:T(128)S(1)} all-reduce(f32[32]{0:T(128)S(1)} %get-tuple-element.48), channel_id=1, replica_groups=mesh['row'=4,'col'=8] {'row','col'}, use_global_device_ids=true, to_apply=%region_11.12 | all-reduce | flops 32 | bytes 256 | tf_op jit(solution)/shard_map/psum | solution.py:55
  333.2 0.0 copy-done
  333.2 0.7 multiply_add_fusion.1
  333.9 0.0 copy-start.1
  333.9 0.0 all-gather.11.cloned.1.call-update
  333.9 53.6 %all-gather.11.cloned.1.call-done = f32[1024,256]{1,0:T(8,128)} async-done(((f32[32,256]{1,0:T(8,128)}), f32[1024,256]{1,0:T(8,128)}) %all-gather.11.cloned.1.call-update) | async-done | bytes 1048592 | tf_op jit(solution)/shard_map/all_gather | solution.py:74
  387.6 1.3 copy.13
  388.9 9.8 %multiply_reduce_fusion.1 = (f32[32]{0:T(128)S(1)}, f32[32,256]{1,0:T(8,128)S(1)}) fusion(f32[32,256]{1,0:T(8,128)} %multiply_add_fusion.1, f32[]{:T(128)} %bitcast.31, f32[32,8192]{1,0:T(8,128)S(1)} %bitcast.34, f32[256,8192]{1,0:T(8,128)} %exponential_multiply_fusion), kind=kOutput, calls=%fused_computation.11 | convolution fusion | flops 805339136 | bytes 9502852 | tf_op jit(solution)/shard_map/while/body/eval_jaxpr/dot_general | solution.py:42
  398.7 39.3 %psum.47 = f32[32]{0:T(128)S(1)} all-reduce(f32[32]{0:T(128)S(1)} %get-tuple-element.63), channel_id=1, replica_groups=mesh['row'=4,'col'=8] {'row','col'}, use_global_device_ids=true, to_apply=%region_13.14 | all-reduce | flops 32 | bytes 256 | tf_op jit(solution)/shard_map/psum | solution.py:77
  438.0 0.0 copy-done.1
  438.0 0.7 multiply_subtract_fusion
  (5 shorter events, 0.0 us)
Async XLA Ops:
  7.2 91.4 %all-gather.7.cloned.1.call-start = ((), (), s32[]{:S(2)}) async-start(), calls=%async_computation | async-start | bytes 1081344 | tf_op jit(solution)/shard_map/all_gather | solution.py:74
  9.3 233.4 %all-gather.9.cloned.1.call-start = ((), (), s32[]{:S(2)}) async-start(), calls=%async_computation.1 | async-start | bytes 1081344 | tf_op jit(solution)/shard_map/all_gather | solution.py:74
  84.5 15.3 %copy-start.2 = (f32[32,256]{1,0:T(8,128)S(1)}, f32[32,256]{1,0:T(8,128)}, u32[]{:S(2)}) copy-start(f32[32,256]{1,0:T(8,128)} %pad_maximum_fusion) | copy-start | bytes 98308
  98.5 48.0 %copy-start.3 = (f32[256]{0:T(256)S(1)}, f32[256]{0:T(256)}, u32[]{:S(2)}) copy-start(f32[256]{0:T(256)} %param.10) | copy-start | bytes 3076
  189.3 143.9 %copy-start = (f32[32,256]{1,0:T(8,128)S(1)}, f32[32,256]{1,0:T(8,128)}, u32[]{:S(2)}) copy-start(f32[32,256]{1,0:T(8,128)} %multiply_add_fusion.2) | copy-start | bytes 98308
  189.3 198.2 %all-gather.11.cloned.1.call-start = ((), (), s32[]{:S(2)}) async-start(), calls=%async_computation.2 | async-start | bytes 1081344 | tf_op jit(solution)/shard_map/all_gather | solution.py:74
  333.9 104.1 %copy-start.1 = (f32[32,256]{1,0:T(8,128)S(1)}, f32[32,256]{1,0:T(8,128)}, u32[]{:S(2)}) copy-start(f32[32,256]{1,0:T(8,128)} %multiply_add_fusion.1) | copy-start | bytes 98308
Sparse Core Ops, SparseCore 0:
  11.6 56.4 all-gather.6
  189.5 53.1 all-gather.8
  334.0 53.4 all-gather.10
